TPU v7x, 32 devices: a whole 2x2x4 slice. The times are simulated.
32 devices in a mesh: rep: 2 (over y), seq: 4 (over z), head: 2 (over x), sub: 2 (over core).
Axes of the slice: x: 2, y: 2, z: 4, core: 2. Of those that a mesh axis runs over, the one named last changes fastest.
Arguments:
- tokens: bfloat16 [32, 4096], P(('rep', 'sub'), 'seq'), parts along dimension 0, may hold values from -260 to 260
- attn_gain: float32 [4096], P('seq'), may hold values from 0.1 to 1.9
- w_query: bfloat16 [4096, 4096], P('seq', 'head'), may hold values from -0.09375 to 0.09375
- key_projection_weight: bfloat16 [4096, 1024], P('seq', 'head'), may hold values from -0.375 to 0.375
- value_projection_weight: bfloat16 [4096, 1024], P('seq', 'head'), may hold values from -0.375 to 0.375
- w_attn_out: bfloat16 [4096, 4096], P('head', 'seq'), may hold values from -0.09375 to 0.09375
- cache_keys: bfloat16 [32, 8, 2048, 128], P(('rep', 'sub'), 'head', 'seq'), parts along dimension 0, may hold values from -2500 to 2500
- stored_value_cache: bfloat16 [32, 8, 2048, 128], P(('rep', 'sub'), 'head', 'seq'), parts along dimension 0, may hold values from -12 to 12
- lengths: int32 [32], P(('rep', 'sub')), parts along dimension 0, may hold values from 1024 to 2048
- positions: int32 [32], P(('rep', 'sub')), parts along dimension 0, may hold values from 0 to 2047
- mamba_gain: float32 [4096], replicated, may hold values from 0.1 to 1.9
- w_in: bfloat16 [2, 4096, 8192], P(None, None, ('seq', 'head')), may hold values from -0.09375 to 0.09375
- conv_weight: float32 [4, 8192], P(None, ('seq', 'head')), may hold values from -3 to 3
- conv_bias: float32 [8192], P(('seq', 'head')), may hold values from -0.5 to 0.5
- conv_state: float32 [32, 3, 8192], P(('rep', 'sub'), None, ('seq', 'head')), parts along dimension 0, may hold values from -6 to 6
- w_xproj: bfloat16 [8192, 288], P(('seq', 'head')), may hold values from -0.0625 to 0.0625
- w_dt: bfloat16 [256, 8192], P(None, ('seq', 'head')), may hold values from -0.375 to 0.375
- dt_bias: float32 [8192], P(('seq', 'head')), may hold values from -4 to 0
- a_log: float32 [16, 8192], P(None, ('seq', 'head')), may hold values from 0 to 2.77
- skip_gain: float32 [8192], P(('seq', 'head')), may hold values from 0.25 to 2
- ssm_state: float32 [32, 16, 8192], P(('rep', 'sub'), None, ('seq', 'head')), parts along dimension 0, may hold values from -6 to 6
- w_mamba_out: bfloat16 [8192, 4096], P(('seq', 'head')), may hold values from -0.09375 to 0.09375
Outputs:
- hidden_out: bfloat16 [32, 4096], P(('rep', 'sub'), 'seq'), parts along dimension 0
- new_state: float32 [32, 16, 8192], P(('rep', 'sub'), None, ('seq', 'head')), parts along dimension 0
There are 2 independent parts, one for each index of `rep`. A program takes and returns all parts, laid end to end along the dimension named above; an argument that names none is the same for every part. Nothing has to cross between parts.
Inputs may be any that keep to these rules, and one draw needn't show every extreme that they name: Cache positions p < lengths[b] hold sequence b's past keys and values; later positions are not attended.
All inputs are finite; a program needn't handle non-finite values.
Results may differ from a plain program's by a relative error of at most 0.015.
Values may be sent and summed in bfloat16 or wider, within the bound.
No kernel may reach another device: no remote copies, remote signals or barrier semaphores. Data moves between devices by JAX's collectives and lax.ppermute only.
A program may use at most 128 MiB of HBM per device.

v0:
```python
import functools
import math

import jax
import jax.numpy as jnp
from jax import lax
from jax.experimental import pallas as pl
from jax.experimental.pallas import tpu as pltpu
from jax.sharding import PartitionSpec as P


norm_eps = 1e-05
masked_floor = -1e30
rope_base = 10000.0
group_axes = ("seq", "head")


def paired(count):
    return count & (count - 1) == 0 and count <= 4


def partner(index, step, count):
    if paired(count):
        return lax.bitwise_xor(index, step)
    return lax.rem(index + step, count)


def from_partners(values, axis):
    count = lax.axis_size(axis)
    result = []
    for k in range(1, count):
        pairs = [(i, i ^ k if paired(count) else (i + k) % count) for i in range(count)]
        result.append(held(lax.ppermute(values[k - 1], axis, pairs)))
    return result


def from_group(value):
    return lax.all_to_all(value, group_axes, 0, 0, tiled=False)


f32 = jnp.float32
bf16 = jnp.bfloat16
LANES = 128
WEIGHT = 10**12
in_vmem = pl.BlockSpec(memory_space=pltpu.VMEM)
in_smem = pl.BlockSpec(memory_space=pltpu.SMEM)
in_any = pl.BlockSpec(memory_space=pl.ANY)


def held(value):
    return pltpu.with_memory_space_constraint(value, pltpu.VMEM)


def far(value):
    return pltpu.with_memory_space_constraint(value, pltpu.HBM)


def call(kernel, out_shape, operands, limit, scratch=(), spaces=None, aliases={}):
    size = sum(math.prod(x.shape) * x.dtype.itemsize for x in operands)
    return pl.pallas_call(
        kernel,
        out_shape=out_shape,
        in_specs=spaces or [in_vmem] * len(operands),
        out_specs=jax.tree.map(lambda _: in_vmem, out_shape),
        scratch_shapes=scratch,
        input_output_aliases=aliases,
        cost_estimate=pl.CostEstimate(flops=WEIGHT, bytes_accessed=size, transcendentals=0),
        compiler_params=pltpu.CompilerParams(vmem_limit_bytes=limit),
    )(*operands)


def column(ref, rows):
    row = lax.broadcasted_iota(jnp.int32, (rows, LANES), 0)
    result = jnp.zeros((rows, LANES), jnp.int32)
    for b in range(rows):
        result = jnp.where(row == b, ref[b], result)
    return result


def in_three(value):
    high = value.astype(bf16).astype(f32)
    rest = value - high
    middle = rest.astype(bf16).astype(f32)
    return high, middle, rest - middle


def project_kernel(chunks, share, count, tok, gain, positions, wq, wk, wv, *refs):
    outs, scratch = refs[:-7], refs[-7:]
    sents = outs[: count - 1]
    part, fresh, square, cosine, sine = outs[count - 1 :]
    tok_buf, gain_buf, positions_buf, wq_buf, wk_buf, wv_buf, sems = scratch
    rows, cols = tok.shape
    depth = cols // chunks
    head_dim = cosine.shape[1]
    small = []
    pairs = ((tok, tok_buf), (gain, gain_buf), (positions, positions_buf))
    for i, (source, target) in enumerate(pairs):
        small.append(pltpu.make_async_copy(source, target, sems.at[3, i]))
        small[-1].start()
    copies = []
    for c in range(chunks):
        span = pl.ds(c * depth, depth)
        for i, (source, target) in enumerate(((wq, wq_buf), (wk, wk_buf), (wv, wv_buf))):
            copy = pltpu.make_async_copy(source.at[span], target.at[span], sems.at[i, c])
            copy.start()
            copies.append(copy)
    for copy in small:
        copy.wait()
    value = tok_buf[...].astype(f32)
    lifted = (value * gain_buf[...]).astype(bf16)
    squares = jnp.sum(value * value, axis=1, keepdims=True)
    lane = lax.broadcasted_iota(jnp.int32, (rows, LANES), 1)
    high, middle, low = in_three(squares)
    terms = jnp.where(lane == 0, high, jnp.where(lane == 1, middle, jnp.where(lane == 2, low, 0.0)))
    square[...] = jnp.broadcast_to(squares, (rows, LANES))
    half = head_dim // 2
    lane = lax.broadcasted_iota(jnp.int32, (rows, head_dim), 1)
    frequency = jnp.exp(-math.log(rope_base) / half * lax.rem(lane, half).astype(f32))
    angles = column(positions_buf, rows).astype(f32) * frequency
    cosine[...] = jnp.cos(angles)
    sine[...] = jnp.where(lane < half, -1.0, 1.0) * jnp.sin(angles)
    sums = [0.0, 0.0, 0.0]
    for c in range(chunks):
        x = lifted[:, c * depth : (c + 1) * depth]
        for i, buf in enumerate((wq_buf, wk_buf, wv_buf)):
            copies[3 * c + i].wait()
            sums[i] = sums[i] + jnp.dot(
                x, buf[c * depth : (c + 1) * depth], preferred_element_type=f32
            )
    query, key, value = sums
    q_width = query.shape[1]
    part[...] = query
    rounded = query.astype(bf16)
    here = lax.axis_index("seq")

    def pick(total, owner, c):
        result = total[:, :head_dim]
        for h in range(1, total.shape[1] // head_dim):
            block = total[:, h * head_dim : (h + 1) * head_dim]
            result = jnp.where(owner * share + c == h, block, result)
        return result

    for k in range(count):
        owner = here if k == 0 else partner(here, k, count)
        blocks = [pick(total, owner, c) for total in (key, value) for c in range(share)]
        blocks = jnp.concatenate(blocks, axis=1)
        if k == 0:
            fresh[...] = blocks
        else:
            sent = sents[k - 1]
            sent[:, :q_width] = rounded
            sent[:, q_width : q_width + blocks.shape[1]] = blocks.astype(bf16)
            sent[:, q_width + blocks.shape[1] :] = terms.astype(bf16)


def gate_kernel(*refs):
    pass


def attend_kernel(width, share, count, *refs):
    part, fresh, square = refs[:3]
    others = refs[3 : 2 + count]
    cosine, sine, lengths, keys, values = refs[2 + count : 7 + count]
    sent, mean_out, level_out = refs[7 + count :]
    rows, q_width = part.shape
    kv_heads, depth, head_dim = keys.shape[1:]
    heads = q_width // head_dim
    per_kv = heads // kv_heads
    scale = head_dim ** (-0.5)
    here = lax.axis_index("seq")
    squares = square[...]
    for other in others:
        terms = other[:, other.shape[1] - LANES :].astype(f32)
        squares = squares + jnp.sum(terms, axis=1, keepdims=True)
    inv_rms = lax.rsqrt(squares / width + norm_eps)

    def summed(own, own_start, start):
        total = own[:, own_start : own_start + head_dim]
        for other in others:
            total = total + other[:, start : start + head_dim].astype(f32)
        return total * inv_rms

    def rotated(x):
        x = x * cosine[...] + pltpu.roll(x, head_dim // 2, 1) * sine[...]
        return x.astype(bf16).astype(f32)

    tall = per_kv * rows
    owner = lax.rem(lax.broadcasted_iota(jnp.int32, (tall, depth), 0), rows)
    narrow = lax.rem(lax.broadcasted_iota(jnp.int32, (tall, head_dim), 0), rows)
    slot = lax.broadcasted_iota(jnp.int32, (tall, depth), 1)
    limit = column(lengths, rows)[:, :1] - here * depth
    live = slot < jnp.concatenate([limit] * per_kv, axis=0)
    lane = lax.broadcasted_iota(jnp.int32, (rows, LANES), 1)
    new_keys = []
    new_values = []
    for c in range(share):
        start = c * head_dim
        x = rotated(summed(fresh, start, q_width + start))
        new_keys.append(jnp.concatenate([x] * per_kv, axis=0))
        start = (share + c) * head_dim
        x = summed(fresh, start, q_width + start).astype(bf16).astype(f32)
        new_values.append(jnp.concatenate([x] * per_kv, axis=0))
    levels = jnp.zeros((rows, LANES), f32)
    together = 2 if kv_heads % 2 == 0 else 1
    for base in range(0, kv_heads, together):
        weights, tops, news, totals = [], [], [], []
        for h in range(base, base + together):
            stacked = [
                rotated(summed(part, start, start))
                for start in range(h * per_kv * head_dim, (h + 1) * per_kv * head_dim, head_dim)
            ]
            stacked = jnp.concatenate(stacked, axis=0)
            mine = (here == h // share).astype(f32)
            score_new = jnp.sum(stacked * new_keys[h % share], axis=1, keepdims=True) * scale
            score_new = score_new * mine + masked_floor * (1.0 - mine)
            scores = jnp.zeros((tall, depth), f32)
            for b in range(0, rows, 2):
                both = range(b, min(b + 2, rows))
                left = [jnp.where(narrow == i, stacked, 0.0) for i in both]
                scores = scores + lax.dot_general(
                    jnp.concatenate(left, axis=1).astype(bf16),
                    jnp.concatenate([keys[i, h] for i in both], axis=1),
                    (((1,), (1,)), ((), ())),
                    preferred_element_type=f32,
                )
            scores = jnp.where(live, scores * scale, masked_floor)
            top = jnp.maximum(jnp.max(scores, axis=1, keepdims=True), score_new)
            weight = jnp.where(live, jnp.exp(scores - top), 0.0)
            new = jnp.exp(score_new - top) * mine
            weights.append(weight)
            tops.append(top)
            news.append(new)
            totals.append(jnp.sum(weight, axis=1, keepdims=True) + new)
        acc = jnp.zeros((together * tall, together * head_dim), f32)
        for b in range(rows):
            left = [jnp.where(owner == b, weight, 0.0).astype(bf16) for weight in weights]
            acc = acc + jnp.dot(
                jnp.concatenate(left, axis=0),
                jnp.concatenate([values[b, base + i] for i in range(together)], axis=1),
                preferred_element_type=f32,
            )
        for i in range(together):
            mean = acc[i * tall : (i + 1) * tall, i * head_dim : (i + 1) * head_dim]
            mean = mean + news[i] * new_values[(base + i) % share]
            some = totals[i] > 0.0
            safe = jnp.where(some, totals[i], 1.0)
            level = jnp.where(some, tops[i] + jnp.log(safe), masked_floor)
            mean = mean / safe
            for j in range(per_kv):
                head = (base + i) * per_kv + j
                block = mean[j * rows : (j + 1) * rows]
                mean_out[:, head * head_dim : (head + 1) * head_dim] = block
                sent[:, head * head_dim : (head + 1) * head_dim] = block.astype(bf16)
                levels = jnp.where(lane == head, level[j * rows : (j + 1) * rows], levels)
    level_out[...] = levels
    high, middle, low = in_three(levels)
    packed = high + pltpu.roll(middle, heads, 1) + pltpu.roll(low, 2 * heads, 1)
    sent[:, q_width : q_width + LANES] = packed.astype(bf16)


def merge_kernel(heads, count, *refs):
    mean, level = refs[0], refs[1]
    others = refs[2 : 1 + count]
    tok, w_out, out = refs[1 + count :]
    _, q_width = mean.shape
    head_dim = q_width // heads
    levels = [level[...]]
    for other in others:
        packed = other[:, q_width : q_width + LANES].astype(f32)
        levels.append(
            (packed + pltpu.roll(packed, LANES - heads, 1))
            + pltpu.roll(packed, LANES - 2 * heads, 1)
        )
    top = functools.reduce(jnp.maximum, levels)
    factors = [jnp.exp(x - top) for x in levels]
    total = functools.reduce(jnp.add, factors)
    factors = [x / total for x in factors]
    blocks = []
    for j in range(heads):
        span = slice(j * head_dim, (j + 1) * head_dim)
        terms = [mean[:, span]] + [other[:, span].astype(f32) for other in others]
        block = 0.0
        for factor, term in zip(factors, terms):
            block = block + factor[:, j : j + 1] * term
        blocks.append(block.astype(bf16))
    attended = jnp.concatenate(blocks, axis=1)
    part = jnp.dot(attended, w_out[...], preferred_element_type=f32)
    first = (lax.axis_index("head") == 0).astype(f32)
    part = (part + tok[...].astype(f32) * first).astype(bf16)
    for g in range(out.shape[0]):
        out[g] = part


def mix_kernel(head_size, pieces, gain, w_in, taps, bias, state, w_xproj, *outs):
    proj, u_out, gate_out, mid_out = outs
    group, _, cols = pieces.shape
    blocks = []
    squares = 0.0
    for s in range(group // head_size):
        block = pieces[s * head_size].astype(f32)
        for h in range(1, head_size):
            block = block + pieces[s * head_size + h].astype(f32)
        blocks.append(block)
        squares = squares + jnp.sum(block * block, axis=1, keepdims=True)
    here = lax.axis_index("seq")
    own = blocks[0]
    for s in range(1, len(blocks)):
        own = jnp.where(here == s, blocks[s], own)
    mid_out[...] = own
    inv_rms = lax.rsqrt(squares / (cols * len(blocks)) + norm_eps)
    inner = 0.0
    gate = 0.0
    for s, block in enumerate(blocks):
        span = slice(s * cols, (s + 1) * cols)
        lifted = (block * inv_rms * gain[:, span]).astype(bf16)
        inner = inner + jnp.dot(lifted, w_in[0, span], preferred_element_type=f32)
        gate = gate + jnp.dot(lifted, w_in[1, span], preferred_element_type=f32)
    last = state.shape[0]
    mixed = inner * taps[last : last + 1, :] + bias[...]
    for k in range(last):
        mixed = mixed + state[k] * taps[k : k + 1, :]
    active = mixed / (1.0 + jnp.exp(-mixed))
    u_out[...] = active
    gate_out[...] = gate / (1.0 + jnp.exp(-gate))
    part = lax.dot_general(
        active.astype(bf16), w_xproj[...], (((1,), (1,)), ((), ())), preferred_element_type=f32
    )
    for g in range(proj.shape[0]):
        proj[g] = part


def state_kernel(
    head_size, pieces, w_dt, dt_bias, a_log, skip, state, u, gate, w_out, new_state, out
):
    rows, states, _ = state.shape
    rank = w_dt.shape[0]
    total = pieces[0]
    for g in range(1, pieces.shape[0]):
        total = total + pieces[g]
    maps = total[:, rank : rank + 2 * states]
    maps = jnp.concatenate([maps, jnp.zeros((rows, LANES - 2 * states), f32)], axis=1)
    maps = jnp.concatenate([maps, jnp.zeros((LANES - rows, LANES), f32)], axis=0).T
    raw = (
        jnp.dot(total[:, :rank].astype(bf16), w_dt[...], preferred_element_type=f32) + dt_bias[...]
    )
    step = jnp.maximum(raw, 0.0) + jnp.log1p(jnp.exp(-jnp.abs(raw)))
    rate = -jnp.exp(a_log[...])
    active = u[...]
    scaled = step * active
    lines = []
    for b in range(rows):
        fresh = jnp.exp(step[b : b + 1] * rate) * state[b] + scaled[b : b + 1] * maps[:states, b : b + 1]
        new_state[b] = fresh
        lines.append(jnp.sum(fresh * maps[states : 2 * states, b : b + 1], axis=0, keepdims=True))
    readout = jnp.concatenate(lines, axis=0) + skip[...] * active
    gated = (readout * gate[...]).astype(bf16)
    cols = out.shape[2]
    for s in range(out.shape[0] // head_size):
        part = jnp.dot(
            gated, w_out[:, s * cols : (s + 1) * cols], preferred_element_type=f32
        ).astype(bf16)
        for h in range(head_size):
            out[s * head_size + h] = part


def finish_kernel(mid, pieces, out):
    total = pieces[0].astype(f32)
    for g in range(1, pieces.shape[0]):
        total = total + pieces[g].astype(f32)
    out[...] = (mid[...] + total).astype(bf16)


def local(
    tokens,
    attn_gain,
    w_query,
    key_projection_weight,
    value_projection_weight,
    w_attn_out,
    cache_keys,
    stored_value_cache,
    lengths,
    positions,
    mamba_gain,
    w_in,
    conv_weight,
    conv_bias,
    conv_state,
    w_xproj,
    w_dt,
    dt_bias,
    a_log,
    skip_gain,
    ssm_state,
    w_mamba_out,
):
    shape = jax.ShapeDtypeStruct
    mib = 2**20
    rows, cols = tokens.shape
    head_dim = cache_keys.shape[3]
    kv_heads = cache_keys.shape[1]
    q_width = w_query.shape[1]
    heads = q_width // head_dim
    seq_size = lax.axis_size("seq")
    head_size = lax.axis_size("head")
    group = seq_size * head_size
    width = cols * seq_size
    channels = w_dt.shape[1]
    mapped = w_xproj.shape[1]

    chunks = 4
    share = -(-kv_heads // seq_size)
    owned = 2 * share * head_dim
    *sents, part, fresh, square, cosine, sine = call(
        functools.partial(project_kernel, chunks, share, seq_size),
        tuple(pltpu.VMEM((rows, q_width + owned + LANES), bf16) for _ in range(1, seq_size))
        + (
            shape((rows, q_width), f32),
            shape((rows, owned), f32),
            shape((rows, LANES), f32),
            shape((rows, head_dim), f32),
            shape((rows, head_dim), f32),
        ),
        (
            far(tokens),
            far(attn_gain[None]),
            far(positions),
            far(w_query),
            far(key_projection_weight),
            far(value_projection_weight),
        ),
        10 * mib,
        scratch=[
            pltpu.VMEM(tokens.shape, bf16),
            pltpu.VMEM((1, cols), f32),
            pltpu.SMEM(positions.shape, jnp.int32),
            pltpu.VMEM(w_query.shape, bf16),
            pltpu.VMEM(key_projection_weight.shape, bf16),
            pltpu.VMEM(value_projection_weight.shape, bf16),
            pltpu.SemaphoreType.DMA((4, chunks)),
        ],
        spaces=[in_any] * 6,
    )
    sents = call(
        gate_kernel,
        tuple(pltpu.VMEM(x.shape, x.dtype) for x in sents),
        tuple(held(x) for x in sents),
        mib,
        aliases={i: i for i in range(len(sents))},
    )
    others = from_partners(sents, "seq")
    sent, mean, level = call(
        functools.partial(attend_kernel, width, share, seq_size),
        (
            shape((rows, q_width + LANES), bf16),
            shape((rows, q_width), f32),
            shape((rows, LANES), f32),
        ),
        (part, fresh, square, *others, cosine, sine, lengths, cache_keys, stored_value_cache),
        LIMITS[0] * mib,
        spaces=[in_vmem] * (4 + seq_size) + [in_smem, in_vmem, in_vmem],
    )
    others = from_partners([sent] * (seq_size - 1), "seq")
    (out,) = call(
        functools.partial(merge_kernel, heads, seq_size),
        (shape((group, rows, cols), bf16),),
        (mean, level, *others, tokens, w_attn_out),
        LIMITS[1] * mib,
    )
    pieces = from_group(out)
    proj, active, gate, mid = call(
        functools.partial(mix_kernel, head_size),
        (
            shape((group, rows, mapped), f32),
            shape((rows, channels), f32),
            shape((rows, channels), f32),
            shape((rows, cols), f32),
        ),
        (
            pieces,
            mamba_gain[None],
            w_in,
            conv_weight,
            conv_bias[None],
            conv_state.transpose(1, 0, 2),
            w_xproj.T,
        ),
        LIMITS[2] * mib,
    )
    new_state, out = call(
        functools.partial(state_kernel, head_size),
        (shape(ssm_state.shape, f32), shape((group, rows, cols), bf16)),
        (
            from_group(proj),
            w_dt,
            dt_bias[None],
            a_log,
            skip_gain[None],
            ssm_state,
            active,
            gate,
            w_mamba_out,
        ),
        LIMITS[3] * mib,
    )
    (hidden_out,) = call(
        finish_kernel, (shape((rows, cols), bf16),), (mid, from_group(out)), 2 * mib
    )
    return (hidden_out, new_state)


LIMITS = (4, 4, 4, 4)


def solution(mesh):
    in_specs = (
        P(("rep", "sub"), "seq"),
        P("seq"),
        P("seq", "head"),
        P("seq", "head"),
        P("seq", "head"),
        P("head", "seq"),
        P(("rep", "sub"), "head", "seq", None),
        P(("rep", "sub"), "head", "seq", None),
        P(("rep", "sub")),
        P(("rep", "sub")),
        P(),
        P(None, None, ("seq", "head")),
        P(None, ("seq", "head")),
        P(("seq", "head")),
        P(("rep", "sub"), None, ("seq", "head")),
        P(("seq", "head"), None),
        P(None, ("seq", "head")),
        P(("seq", "head")),
        P(None, ("seq", "head")),
        P(("seq", "head")),
        P(("rep", "sub"), None, ("seq", "head")),
        P(("seq", "head"), None),
    )
    out_specs = (P(("rep", "sub"), "seq"), P(("rep", "sub"), None, ("seq", "head")))
    return jax.shard_map(local, mesh=mesh, in_specs=in_specs, out_specs=out_specs, check_vma=False)
```

profile of v0, /device:TPU:0, one launch (start us, length us, event | category | flops | bytes accessed | tf_op | source)
XLA Modules:
  0.0 62.7 jit_solution(17878406051933288536)
XLA Ops:
  0.6 3.4 %shard_map.221 = (bf16[8,2432]{1,0:T(8,128)(2,1)S(1)}, bf16[8,2432]{1,0:T(8,128)(2,1)S(1)}, bf16[8,2432]{1,0:T(8,128)(2,1)S(1)}, f32[8,2048]{1,0:T(8,128)S(1)}, ...) custom-call(bf16[8,1024]{1,0:T(8,128)(2,1)} %refs_5_.1, ...), custom_call_target="tpu_custom_call" | custom-call | flops 999999995904 | bytes 6311968 | tf_op jit(solution)/shard_map/pallas_call | solution.py:60
  4.0 0.0 copy-start.2
  4.0 0.0 copy-start.3
  4.0 0.0 copy-start.16
  4.1 3.1 %collective-permute-start = (bf16[8,2432]{1,0:T(8,128)(2,1)S(1)}, bf16[8,2432]{1,0:T(8,128)(2,1)S(1)}, u32[]{:S(2)}, u32[]{:S(2)}) collective-permute-start(bf16[8,2432]{1,0:T(8,128)(2,1)S(1)} %get-tuple-element.28), channel_id=1, source_target_pairs={{0,4},{4,0},{8,12},{12,8},{1,5},{5,1},{9,13},{13,9},{2,6},{6,2},{1... | collective-permute-start | bytes 116744 | tf_op jit(solution)/shard_map/ppermute | solution.py:33
  7.2 2.6 %collective-permute-start.1 = (bf16[8,2432]{1,0:T(8,128)(2,1)S(1)}, bf16[8,2432]{1,0:T(8,128)(2,1)S(1)}, u32[]{:S(2)}, u32[]{:S(2)}) collective-permute-start(bf16[8,2432]{1,0:T(8,128)(2,1)S(1)} %get-tuple-element.29), channel_id=1, source_target_pairs={{0,8},{4,12},{8,0},{12,4},{1,9},{5,13},{9,1},{13,5},{2,10},{6,14},... | collective-permute-start | bytes 116744 | tf_op jit(solution)/shard_map/ppermute | solution.py:33
  9.8 3.0 %collective-permute-done.1.refs_4_ = bf16[8,2432]{1,0:T(8,128)(2,1)S(1)} collective-permute-done((bf16[8,2432]{1,0:T(8,128)(2,1)S(1)}, bf16[8,2432]{1,0:T(8,128)(2,1)S(1)}, u32[]{:S(2)}, u32[]{:S(2)}) %collective-permute-start.1) | collective-permute-done | bytes 38944 | tf_op jit(solution)/shard_map/ppermute | solution.py:33
  12.8 2.8 %collective-permute-done.2.refs_5_ = bf16[8,2432]{1,0:T(8,128)(2,1)S(1)} collective-permute-done((bf16[8,2432]{1,0:T(8,128)(2,1)S(1)}, bf16[8,2432]{1,0:T(8,128)(2,1)S(1)}, u32[]{:S(2)}, u32[]{:S(2)}) %collective-permute-start.2) | collective-permute-done | bytes 38944 | tf_op jit(solution)/shard_map/ppermute | solution.py:33
  15.6 0.0 copy-start.4
  15.6 0.0 copy-start.10
  15.6 3.0 %shard_map.223 = (bf16[8,2176]{1,0:T(8,128)(2,1)S(1)}, f32[8,2048]{1,0:T(8,128)S(1)}, f32[8,128]{1,0:T(8,128)S(1)}) custom-call(f32[8,2048]{1,0:T(8,128)S(1)} %get-tuple-element.22.refs_0_, f32[8,256]{1,0:T(8,128)S(1)} %get-tuple-element.23.refs_1_, f32[8,128]{1,0:T(8,128)S(1)} %get-tuple-element.24.refs_2_, ...), custom_call_target="tpu_custom_call" | custom-call | flops 999999995904 | bytes 8591392 | tf_op jit(solution)/shard_map/pallas_call | solution.py:60
  18.6 0.6 collective-permute-start.5
  19.1 0.0 collective-permute-start.4
  19.2 3.9 %collective-permute-start.3 = (bf16[8,2176]{1,0:T(8,128)(2,1)S(1)}, bf16[8,2176]{1,0:T(8,128)(2,1)S(1)}, u32[]{:S(2)}, u32[]{:S(2)}) collective-permute-start(bf16[8,2176]{1,0:T(8,128)(2,1)S(1)} %get-tuple-element.35), channel_id=1, source_target_pairs={{0,4},{4,0},{8,12},{12,8},{1,5},{5,1},{9,13},{13,9},{2,6},{6,2},{1... | collective-permute-start | bytes 104456 | tf_op jit(solution)/shard_map/ppermute | solution.py:33
  23.0 1.3 %collective-permute-done.5.refs_4_ = bf16[8,2176]{1,0:T(8,128)(2,1)S(1)} collective-permute-done((bf16[8,2176]{1,0:T(8,128)(2,1)S(1)}, bf16[8,2176]{1,0:T(8,128)(2,1)S(1)}, u32[]{:S(2)}, u32[]{:S(2)}) %collective-permute-start.5) | collective-permute-done | bytes 34848 | tf_op jit(solution)/shard_map/ppermute | solution.py:33
  24.4 0.6 collective-permute-done.3.refs_2_
  24.9 0.0 copy-start.8
  25.0 0.0 copy-start.11
  25.0 0.0 copy-start.12
  25.0 0.0 copy-start.13
  25.0 0.8 %shard_map.224 = bf16[8,8,1024]{2,1,0:T(8,128)(2,1)S(1)} custom-call(f32[8,2048]{1,0:T(8,128)S(1)} %get-tuple-element.33.refs_0_, f32[8,128]{1,0:T(8,128)S(1)} %get-tuple-element.34.refs_1_, bf16[8,2176]{1,0:T(8,128)(2,1)S(1)} %collective-permute-done.3.refs_2_, bf16[8,2176]{1,0:T(8,128)(2,1)S(1)} %collective-permute-done.4.refs_3_, ...), custom_call_target="tpu_custom_call" | custom-call | flops 999999995904 | bytes 4384768 | tf_op jit(solution)/shard_map/pallas_call | solution.py:60
  25.8 12.0 %all_to_all.15.pieces = bf16[8,8,1024]{2,1,0:T(8,128)(2,1)S(1)} all-to-all(bf16[8,8,1024]{2,1,0:T(8,128)(2,1)S(1)} %shard_map.224), channel_id=1, replica_groups=mesh['rep'=2,'seq'=4,'head'=2,'sub'=2] {'seq','head'}, dimensions={0} | all-to-all | bytes 262144 | tf_op jit(solution)/shard_map/all_to_all | solution.py:38
  37.8 0.0 copy-start.1
  37.8 0.0 copy-start.6
  37.8 0.0 copy-start.7
  37.9 0.0 copy-start.14
  37.9 0.0 copy-start.15
  37.9 2.5 %shard_map.225 = (f32[8,8,288]{2,1,0:T(8,128)S(1)}, f32[8,1024]{1,0:T(8,128)S(1)}, f32[8,1024]{1,0:T(8,128)S(1)}, f32[8,1024]{1,0:T(8,128)S(1)}) custom-call(bf16[8,8,1024]{2,1,0:T(8,128)(2,1)S(1)} %all_to_all.15.pieces, f32[1,4096]{1,0:T(1,128)S(1)} %bitcast.9, bf16[2,4096,1024]{2,1,0:T(8,128)(2,1)S(1)} %copy-done, f32[4,1024]{1,0:T(4,128)S(1)} %copy-done.12, ...), custom_call_target="tpu_custom_call" | custom-call | flops 999999995904 | bytes 17633280 | tf_op jit(solution)/shard_map/pallas_call | solution.py:60
  40.4 9.7 %all_to_all.16.pieces = f32[8,8,288]{2,1,0:T(8,128)S(1)} all-to-all(f32[8,8,288]{2,1,0:T(8,128)S(1)} %get-tuple-element.37), channel_id=1, replica_groups=mesh['rep'=2,'seq'=4,'head'=2,'sub'=2] {'seq','head'}, dimensions={0} | all-to-all | bytes 147456 | tf_op jit(solution)/shard_map/all_to_all | solution.py:38
  50.1 2.3 %shard_map.226 = (f32[8,16,1024]{2,1,0:T(8,128)}, bf16[8,8,1024]{2,1,0:T(8,128)(2,1)S(1)}) custom-call(f32[8,8,288]{2,1,0:T(8,128)S(1)} %all_to_all.16.pieces, bf16[256,1024]{1,0:T(8,128)(2,1)S(1)} %copy-done.6, f32[1,1024]{1,0:T(1,128)S(1)} %bitcast.11, f32[16,1024]{1,0:T(8,128)S(1)} %copy-done.9, f32[1,1024]{1,0:T(1,128)S(1)} %bitcast.12, ...), custom_call_target="tpu_custom_call" | custom-call | flops 999999995904 | bytes 9650176 | tf_op jit(solution)/shard_map/pallas_call | solution.py:60
  52.4 9.7 %all_to_all.17.pieces = bf16[8,8,1024]{2,1,0:T(8,128)(2,1)S(1)} all-to-all(bf16[8,8,1024]{2,1,0:T(8,128)(2,1)S(1)} %get-tuple-element.40), channel_id=1, replica_groups=mesh['rep'=2,'seq'=4,'head'=2,'sub'=2] {'seq','head'}, dimensions={0} | all-to-all | bytes 262144 | tf_op jit(solution)/shard_map/all_to_all | solution.py:38
  62.1 0.6 %shard_map.227 = bf16[8,1024]{1,0:T(8,128)(2,1)} custom-call(f32[8,1024]{1,0:T(8,128)S(1)} %get-tuple-element.36.mid, bf16[8,8,1024]{2,1,0:T(8,128)(2,1)S(1)} %all_to_all.17.pieces), custom_call_target="tpu_custom_call" | custom-call | flops 999999995904 | bytes 163840 | tf_op jit(solution)/shard_map/pallas_call | solution.py:60
  (24 shorter events, 0.1 us)
Async XLA Ops:
  4.0 11.5 %copy-start.2 = (bf16[8,4,512,128]{3,2,1,0:T(8,128)(2,1)S(1)}, bf16[8,4,512,128]{3,2,1,0:T(8,128)(2,1)}, u32[]{:S(2)}) copy-start(bf16[8,4,512,128]{3,2,1,0:T(8,128)(2,1)} %refs_9_.1) | copy-start | bytes 12582916
  4.0 11.5 %copy-start.3 = (bf16[8,4,512,128]{3,2,1,0:T(8,128)(2,1)S(1)}, bf16[8,4,512,128]{3,2,1,0:T(8,128)(2,1)}, u32[]{:S(2)}) copy-start(bf16[8,4,512,128]{3,2,1,0:T(8,128)(2,1)} %refs_10_.1) | copy-start | bytes 12582916
  4.0 11.5 %copy-start.16 = (s32[8]{0:T(128)S(1)}, s32[8]{0:T(128)}, u32[]{:S(2)}) copy-start(s32[8]{0:T(128)} %refs_8_.1) | copy-start | bytes 100
  4.1 5.7 %collective-permute-start = (bf16[8,2432]{1,0:T(8,128)(2,1)S(1)}, bf16[8,2432]{1,0:T(8,128)(2,1)S(1)}, u32[]{:S(2)}, u32[]{:S(2)}) collective-permute-start(bf16[8,2432]{1,0:T(8,128)(2,1)S(1)} %get-tuple-element.28), channel_id=1, source_target_pairs={{0,4},{4,0},{8,12},{12,8},{1,5},{5,1},{9,13},{13,9},{2,6},{6,2},{1... | collective-permute-start | bytes 116744 | tf_op jit(solution)/shard_map/ppermute | solution.py:33
  7.2 5.6 %collective-permute-start.1 = (bf16[8,2432]{1,0:T(8,128)(2,1)S(1)}, bf16[8,2432]{1,0:T(8,128)(2,1)S(1)}, u32[]{:S(2)}, u32[]{:S(2)}) collective-permute-start(bf16[8,2432]{1,0:T(8,128)(2,1)S(1)} %get-tuple-element.29), channel_id=1, source_target_pairs={{0,8},{4,12},{8,0},{12,4},{1,9},{5,13},{9,1},{13,5},{2,10},{6,14},... | collective-permute-start | bytes 116744 | tf_op jit(solution)/shard_map/ppermute | solution.py:33
  9.8 5.8 %collective-permute-start.2 = (bf16[8,2432]{1,0:T(8,128)(2,1)S(1)}, bf16[8,2432]{1,0:T(8,128)(2,1)S(1)}, u32[]{:S(2)}, u32[]{:S(2)}) collective-permute-start(bf16[8,2432]{1,0:T(8,128)(2,1)S(1)} %get-tuple-element.30), channel_id=1, source_target_pairs={{0,12},{4,8},{8,4},{12,0},{1,13},{5,9},{9,5},{13,1},{2,14},{6,10},... | collective-permute-start | bytes 116744 | tf_op jit(solution)/shard_map/ppermute | solution.py:33
  15.6 9.4 %copy-start.4 = (bf16[2048,1024]{1,0:T(8,128)(2,1)S(1)}, bf16[2048,1024]{1,0:T(8,128)(2,1)}, u32[]{:S(2)}) copy-start(bf16[2048,1024]{1,0:T(8,128)(2,1)} %refs_6_.1) | copy-start | bytes 12582916
  15.6 9.4 %copy-start.10 = (bf16[8,1024]{1,0:T(8,128)(2,1)S(1)}, bf16[8,1024]{1,0:T(8,128)(2,1)}, u32[]{:S(2)}) copy-start(bf16[8,1024]{1,0:T(8,128)(2,1)} %refs_5_.1) | copy-start | bytes 49156
  18.6 5.8 %collective-permute-start.5 = (bf16[8,2176]{1,0:T(8,128)(2,1)S(1)}, bf16[8,2176]{1,0:T(8,128)(2,1)S(1)}, u32[]{:S(2)}, u32[]{:S(2)}) collective-permute-start(bf16[8,2176]{1,0:T(8,128)(2,1)S(1)} %get-tuple-element.35), channel_id=1, source_target_pairs={{0,12},{4,8},{8,4},{12,0},{1,13},{5,9},{9,5},{13,1},{2,14},{6,10},... | collective-permute-start | bytes 104456 | tf_op jit(solution)/shard_map/ppermute | solution.py:33
  19.1 5.2 %collective-permute-start.4 = (bf16[8,2176]{1,0:T(8,128)(2,1)S(1)}, bf16[8,2176]{1,0:T(8,128)(2,1)S(1)}, u32[]{:S(2)}, u32[]{:S(2)}) collective-permute-start(bf16[8,2176]{1,0:T(8,128)(2,1)S(1)} %get-tuple-element.35), channel_id=1, source_target_pairs={{0,8},{4,12},{8,0},{12,4},{1,9},{5,13},{9,1},{13,5},{2,10},{6,14},... | collective-permute-start | bytes 104456 | tf_op jit(solution)/shard_map/ppermute | solution.py:33
  19.2 5.8 %collective-permute-start.3 = (bf16[8,2176]{1,0:T(8,128)(2,1)S(1)}, bf16[8,2176]{1,0:T(8,128)(2,1)S(1)}, u32[]{:S(2)}, u32[]{:S(2)}) collective-permute-start(bf16[8,2176]{1,0:T(8,128)(2,1)S(1)} %get-tuple-element.35), channel_id=1, source_target_pairs={{0,4},{4,0},{8,12},{12,8},{1,5},{5,1},{9,13},{13,9},{2,6},{6,2},{1... | collective-permute-start | bytes 104456 | tf_op jit(solution)/shard_map/ppermute | solution.py:33
  24.9 12.8 %copy-start = (bf16[2,4096,1024]{2,1,0:T(8,128)(2,1)S(1)}, bf16[2,4096,1024]{2,1,0:T(8,128)(2,1)}, u32[]{:S(2)}) copy-start(bf16[2,4096,1024]{2,1,0:T(8,128)(2,1)} %w_in.1) | copy-start | bytes 50331652
  24.9 12.8 %copy-start.5 = (bf16[1024,288]{0,1:T(8,128)(2,1)S(1)}, bf16[1024,288]{0,1:T(8,128)(2,1)}, u32[]{:S(2)}) copy-start(bf16[1024,288]{0,1:T(8,128)(2,1)} %param.37) | copy-start | bytes 1769476
  24.9 12.8 %copy-start.8 = (f32[8,3,1024]{2,0,1:T(8,128)S(1)}, f32[8,3,1024]{2,0,1:T(8,128)}, u32[]{:S(2)}) copy-start(f32[8,3,1024]{2,0,1:T(8,128)} %param.36) | copy-start | bytes 294916
  25.0 12.8 %copy-start.11 = (f32[4096]{0:T(1024)S(1)}, f32[4096]{0:T(1024)}, u32[]{:S(2)}) copy-start(f32[4096]{0:T(1024)} %param.32) | copy-start | bytes 49156
  25.0 12.8 %copy-start.12 = (f32[4,1024]{1,0:T(4,128)S(1)}, f32[4,1024]{1,0:T(4,128)}, u32[]{:S(2)}) copy-start(f32[4,1024]{1,0:T(4,128)} %taps.1) | copy-start | bytes 49156
  25.0 12.8 %copy-start.13 = (f32[1024]{0:T(1024)S(1)}, f32[1024]{0:T(1024)}, u32[]{:S(2)}) copy-start(f32[1024]{0:T(1024)} %param.35) | copy-start | bytes 12292
  37.8 12.3 %copy-start.1 = (bf16[1024,4096]{1,0:T(8,128)(2,1)S(1)}, bf16[1024,4096]{1,0:T(8,128)(2,1)}, u32[]{:S(2)}) copy-start(bf16[1024,4096]{1,0:T(8,128)(2,1)} %w_out.1) | copy-start | bytes 25165828
  37.8 12.2 %copy-start.6 = (bf16[256,1024]{1,0:T(8,128)(2,1)S(1)}, bf16[256,1024]{1,0:T(8,128)(2,1)}, u32[]{:S(2)}) copy-start(bf16[256,1024]{1,0:T(8,128)(2,1)} %w_dt.1) | copy-start | bytes 1572868
  37.8 12.2 %copy-start.7 = (f32[8,16,1024]{2,1,0:T(8,128)S(1)}, f32[8,16,1024]{2,1,0:T(8,128)}, u32[]{:S(2)}) copy-start(f32[8,16,1024]{2,1,0:T(8,128)} %state.1) | copy-start | bytes 1572868
  37.9 12.2 %copy-start.9 = (f32[16,1024]{1,0:T(8,128)S(1)}, f32[16,1024]{1,0:T(8,128)}, u32[]{:S(2)}) copy-start(f32[16,1024]{1,0:T(8,128)} %a_log.1) | copy-start | bytes 196612
  37.9 12.2 %copy-start.14 = (f32[1024]{0:T(1024)S(1)}, f32[1024]{0:T(1024)}, u32[]{:S(2)}) copy-start(f32[1024]{0:T(1024)} %param.39) | copy-start | bytes 12292
  37.9 12.2 %copy-start.15 = (f32[1024]{0:T(1024)S(1)}, f32[1024]{0:T(1024)}, u32[]{:S(2)}) copy-start(f32[1024]{0:T(1024)} %param.41) | copy-start | bytes 12292
where the time goes:
time: 63.1 us; the launch traced here: 62.7 us
  blocking collectives  31.4 us (50%)
  Pallas kernels  12.5 us (20%)
  starting transfers between devices  10.2 us (16%)
  waiting for transfers between devices  7.69 us (12%)
  between operations  0.84 us (1%)
    all_to_all x3, blocking collectives, from_group(): return lax.all_to_all(value, group_axes, 0, 0, tiled=False)  31.4 us
    pallas_call x7, Pallas kernels, call(): pl.pallas_call(kernel, out_shape=out_shape, in_specs=spaces or [in_vmem]...  12.5 us
    ppermute x6, starting transfers between devices, from_partners(): result.append(held(lax.ppermute(values[k - 1], axis, pairs)))  10.2 us
    ppermute x6, waiting for transfers between devices, from_partners(): result.append(held(lax.ppermute(values[k - 1], axis, pairs)))  7.69 us
  transfers between devices with their start and end apart: 6, of which 4 were waited for; matrix products, arithmetic and copies ran while one was open for 0% of the time, Pallas kernels for 0%

commit v1 on v0

--- a/solution.py
+++ b/solution.py
@@ -42,8 +42,8 @@
 bf16 = jnp.bfloat16
 LANES = 128
 WEIGHT = 10**12
+PIECE = 512
 in_vmem = pl.BlockSpec(memory_space=pltpu.VMEM)
-in_smem = pl.BlockSpec(memory_space=pltpu.SMEM)
 in_any = pl.BlockSpec(memory_space=pl.ANY)
 
 
@@ -84,16 +84,17 @@
     return high, middle, rest - middle
 
 
-def project_kernel(chunks, share, count, tok, gain, positions, wq, wk, wv, *refs):
-    outs, scratch = refs[:-7], refs[-7:]
+def project_kernel(chunks, share, context, tok, gain, positions, lengths, wq, wk, wv, *refs):
+    count = lax.axis_size("seq")
+    outs, scratch = refs[:-8], refs[-8:]
     sents = outs[: count - 1]
-    part, fresh, square, cosine, sine = outs[count - 1 :]
-    tok_buf, gain_buf, positions_buf, wq_buf, wk_buf, wv_buf, sems = scratch
+    part, fresh, square, cosine, sine, limit = outs[count - 1 :]
+    tok_buf, gain_buf, positions_buf, lengths_buf, wq_buf, wk_buf, wv_buf, sems = scratch
     rows, cols = tok.shape
     depth = cols // chunks
     head_dim = cosine.shape[1]
     small = []
-    pairs = ((tok, tok_buf), (gain, gain_buf), (positions, positions_buf))
+    pairs = ((tok, tok_buf), (gain, gain_buf), (positions, positions_buf), (lengths, lengths_buf))
     for i, (source, target) in enumerate(pairs):
         small.append(pltpu.make_async_copy(source, target, sems.at[3, i]))
         small[-1].start()
@@ -119,6 +120,8 @@
     angles = column(positions_buf, rows).astype(f32) * frequency
     cosine[...] = jnp.cos(angles)
     sine[...] = jnp.where(lane < half, -1.0, 1.0) * jnp.sin(angles)
+    here = lax.axis_index("seq")
+    limit[...] = column(lengths_buf, rows) - here * context
     sums = [0.0, 0.0, 0.0]
     for c in range(chunks):
         x = lifted[:, c * depth : (c + 1) * depth]
@@ -131,7 +134,6 @@
     q_width = query.shape[1]
     part[...] = query
     rounded = query.astype(bf16)
-    here = lax.axis_index("seq")
 
     def pick(total, owner, c):
         result = total[:, :head_dim]
@@ -160,7 +162,7 @@
 def attend_kernel(width, share, count, *refs):
     part, fresh, square = refs[:3]
     others = refs[3 : 2 + count]
-    cosine, sine, lengths, keys, values = refs[2 + count : 7 + count]
+    cosine, sine, limit, keys, values = refs[2 + count : 7 + count]
     sent, mean_out, level_out = refs[7 + count :]
     rows, q_width = part.shape
     kv_heads, depth, head_dim = keys.shape[1:]
@@ -188,8 +190,7 @@
     owner = lax.rem(lax.broadcasted_iota(jnp.int32, (tall, depth), 0), rows)
     narrow = lax.rem(lax.broadcasted_iota(jnp.int32, (tall, head_dim), 0), rows)
     slot = lax.broadcasted_iota(jnp.int32, (tall, depth), 1)
-    limit = column(lengths, rows)[:, :1] - here * depth
-    live = slot < jnp.concatenate([limit] * per_kv, axis=0)
+    live = slot < jnp.concatenate([limit[:, :1]] * per_kv, axis=0)
     lane = lax.broadcasted_iota(jnp.int32, (rows, LANES), 1)
     new_keys = []
     new_values = []
@@ -332,7 +333,7 @@
 def state_kernel(
     head_size, pieces, w_dt, dt_bias, a_log, skip, state, u, gate, w_out, new_state, out
 ):
-    rows, states, _ = state.shape
+    rows, states, channels = state.shape
     rank = w_dt.shape[0]
     total = pieces[0]
     for g in range(1, pieces.shape[0]):
@@ -340,25 +341,33 @@
     maps = total[:, rank : rank + 2 * states]
     maps = jnp.concatenate([maps, jnp.zeros((rows, LANES - 2 * states), f32)], axis=1)
     maps = jnp.concatenate([maps, jnp.zeros((LANES - rows, LANES), f32)], axis=0).T
-    raw = (
-        jnp.dot(total[:, :rank].astype(bf16), w_dt[...], preferred_element_type=f32) + dt_bias[...]
-    )
-    step = jnp.maximum(raw, 0.0) + jnp.log1p(jnp.exp(-jnp.abs(raw)))
-    rate = -jnp.exp(a_log[...])
-    active = u[...]
-    scaled = step * active
-    lines = []
-    for b in range(rows):
-        fresh = jnp.exp(step[b : b + 1] * rate) * state[b] + scaled[b : b + 1] * maps[:states, b : b + 1]
-        new_state[b] = fresh
-        lines.append(jnp.sum(fresh * maps[states : 2 * states, b : b + 1], axis=0, keepdims=True))
-    readout = jnp.concatenate(lines, axis=0) + skip[...] * active
-    gated = (readout * gate[...]).astype(bf16)
+    low = total[:, :rank].astype(bf16)
     cols = out.shape[2]
-    for s in range(out.shape[0] // head_size):
-        part = jnp.dot(
-            gated, w_out[:, s * cols : (s + 1) * cols], preferred_element_type=f32
-        ).astype(bf16)
+    parts = [0.0] * (out.shape[0] // head_size)
+    piece = min(channels, PIECE)
+    for start in range(0, channels, piece):
+        span = slice(start, start + piece)
+        raw = jnp.dot(low, w_dt[:, span], preferred_element_type=f32) + dt_bias[:, span]
+        step = jnp.maximum(raw, 0.0) + jnp.log1p(jnp.exp(-jnp.abs(raw)))
+        rate = -jnp.exp(a_log[:, span])
+        active = u[:, span]
+        scaled = step * active
+        lines = []
+        for b in range(rows):
+            fresh = jnp.exp(step[b : b + 1] * rate) * state[b, :, span]
+            fresh = fresh + scaled[b : b + 1] * maps[:states, b : b + 1]
+            new_state[b, :, span] = fresh
+            lines.append(
+                jnp.sum(fresh * maps[states : 2 * states, b : b + 1], axis=0, keepdims=True)
+            )
+        readout = jnp.concatenate(lines, axis=0) + skip[:, span] * active
+        gated = (readout * gate[:, span]).astype(bf16)
+        for s in range(len(parts)):
+            parts[s] = parts[s] + jnp.dot(
+                gated, w_out[span, s * cols : (s + 1) * cols], preferred_element_type=f32
+            )
+    for s, part in enumerate(parts):
+        part = part.astype(bf16)
         for h in range(head_size):
             out[s * head_size + h] = part
 
@@ -399,6 +408,7 @@
     rows, cols = tokens.shape
     head_dim = cache_keys.shape[3]
     kv_heads = cache_keys.shape[1]
+    depth = cache_keys.shape[2]
     q_width = w_query.shape[1]
     heads = q_width // head_dim
     seq_size = lax.axis_size("seq")
@@ -411,8 +421,8 @@
     chunks = 4
     share = -(-kv_heads // seq_size)
     owned = 2 * share * head_dim
-    *sents, part, fresh, square, cosine, sine = call(
-        functools.partial(project_kernel, chunks, share, seq_size),
+    *sents, part, fresh, square, cosine, sine, limit = call(
+        functools.partial(project_kernel, chunks, share, depth),
         tuple(pltpu.VMEM((rows, q_width + owned + LANES), bf16) for _ in range(1, seq_size))
         + (
             shape((rows, q_width), f32),
@@ -420,11 +430,13 @@
             shape((rows, LANES), f32),
             shape((rows, head_dim), f32),
             shape((rows, head_dim), f32),
+            shape((rows, LANES), jnp.int32),
         ),
         (
             far(tokens),
             far(attn_gain[None]),
             far(positions),
+            far(lengths),
             far(w_query),
             far(key_projection_weight),
             far(value_projection_weight),
@@ -434,12 +446,13 @@
             pltpu.VMEM(tokens.shape, bf16),
             pltpu.VMEM((1, cols), f32),
             pltpu.SMEM(positions.shape, jnp.int32),
+            pltpu.SMEM(lengths.shape, jnp.int32),
             pltpu.VMEM(w_query.shape, bf16),
             pltpu.VMEM(key_projection_weight.shape, bf16),
             pltpu.VMEM(value_projection_weight.shape, bf16),
             pltpu.SemaphoreType.DMA((4, chunks)),
         ],
-        spaces=[in_any] * 6,
+        spaces=[in_any] * 7,
     )
     sents = call(
         gate_kernel,
@@ -456,9 +469,8 @@
             shape((rows, q_width), f32),
             shape((rows, LANES), f32),
         ),
-        (part, fresh, square, *others, cosine, sine, lengths, cache_keys, stored_value_cache),
+        (part, fresh, square, *others, cosine, sine, limit, cache_keys, stored_value_cache),
         LIMITS[0] * mib,
-        spaces=[in_vmem] * (4 + seq_size) + [in_smem, in_vmem, in_vmem],
     )
     others = from_partners([sent] * (seq_size - 1), "seq")
     (out,) = call(

time: 63.1 us -> 61.8 us (0.979)
  Pallas kernels: 12.5 us -> 11.3 us
    pallas_call x7, Pallas kernels: 12.5 us -> 11.3 us  [call(): pl.pallas_call(kernel, out_shape=out_shape, in_specs=spaces or [in_vmem]...]
where the time goes in v1:
time: 61.8 us; the launch traced here: 61.5 us
  blocking collectives  31.4 us (51%)
  Pallas kernels  11.3 us (18%)
  starting transfers between devices  10.2 us (17%)
  waiting for transfers between devices  7.69 us (12%)
  between operations  0.82 us (1%)
    all_to_all x3, blocking collectives, from_group(): return lax.all_to_all(value, group_axes, 0, 0, tiled=False)  31.4 us
    pallas_call x7, Pallas kernels, call(): pl.pallas_call(kernel, out_shape=out_shape, in_specs=spaces or [in_vmem]...  11.3 us
    ppermute x6, starting transfers between devices, from_partners(): result.append(held(lax.ppermute(values[k - 1], axis, pairs)))  10.2 us
    ppermute x6, waiting for transfers between devices, from_partners(): result.append(held(lax.ppermute(values[k - 1], axis, pairs)))  7.69 us
  transfers between devices with their start and end apart: 6, of which 4 were waited for; matrix products, arithmetic and copies ran while one was open for 0% of the time, Pallas kernels for 0%

profile of v1, /device:TPU:0, one launch (start us, length us, event | category | flops | bytes accessed | tf_op | source)
XLA Modules:
  0.0 61.5 jit_solution(13028931267494723705)
XLA Ops:
  0.6 3.4 %shard_map.221 = (bf16[8,2432]{1,0:T(8,128)(2,1)S(1)}, bf16[8,2432]{1,0:T(8,128)(2,1)S(1)}, bf16[8,2432]{1,0:T(8,128)(2,1)S(1)}, f32[8,2048]{1,0:T(8,128)S(1)}, ...) custom-call(bf16[8,1024]{1,0:T(8,128)(2,1)} %refs_5_.1, ...), custom_call_target="tpu_custom_call" | custom-call | flops 999999995904 | bytes 6312000 | tf_op jit(solution)/shard_map/pallas_call | solution.py:60
  4.0 0.0 copy-start.2
  4.0 0.0 copy-start.3
  4.1 3.1 %collective-permute-start = (bf16[8,2432]{1,0:T(8,128)(2,1)S(1)}, bf16[8,2432]{1,0:T(8,128)(2,1)S(1)}, u32[]{:S(2)}, u32[]{:S(2)}) collective-permute-start(bf16[8,2432]{1,0:T(8,128)(2,1)S(1)} %get-tuple-element.29), channel_id=1, source_target_pairs={{0,4},{4,0},{8,12},{12,8},{1,5},{5,1},{9,13},{13,9},{2,6},{6,2},{1... | collective-permute-start | bytes 116744 | tf_op jit(solution)/shard_map/ppermute | solution.py:33
  7.2 2.6 %collective-permute-start.1 = (bf16[8,2432]{1,0:T(8,128)(2,1)S(1)}, bf16[8,2432]{1,0:T(8,128)(2,1)S(1)}, u32[]{:S(2)}, u32[]{:S(2)}) collective-permute-start(bf16[8,2432]{1,0:T(8,128)(2,1)S(1)} %get-tuple-element.30), channel_id=1, source_target_pairs={{0,8},{4,12},{8,0},{12,4},{1,9},{5,13},{9,1},{13,5},{2,10},{6,14},... | collective-permute-start | bytes 116744 | tf_op jit(solution)/shard_map/ppermute | solution.py:33
  9.8 0.0 collective-permute-start.2
  9.8 0.0 collective-permute-done.refs_3_
  9.8 3.0 %collective-permute-done.1.refs_4_ = bf16[8,2432]{1,0:T(8,128)(2,1)S(1)} collective-permute-done((bf16[8,2432]{1,0:T(8,128)(2,1)S(1)}, bf16[8,2432]{1,0:T(8,128)(2,1)S(1)}, u32[]{:S(2)}, u32[]{:S(2)}) %collective-permute-start.1) | collective-permute-done | bytes 38944 | tf_op jit(solution)/shard_map/ppermute | solution.py:33
  12.8 2.8 %collective-permute-done.2.refs_5_ = bf16[8,2432]{1,0:T(8,128)(2,1)S(1)} collective-permute-done((bf16[8,2432]{1,0:T(8,128)(2,1)S(1)}, bf16[8,2432]{1,0:T(8,128)(2,1)S(1)}, u32[]{:S(2)}, u32[]{:S(2)}) %collective-permute-start.2) | collective-permute-done | bytes 38944 | tf_op jit(solution)/shard_map/ppermute | solution.py:33
  15.6 2.4 %shard_map.223 = (bf16[8,2176]{1,0:T(8,128)(2,1)S(1)}, f32[8,2048]{1,0:T(8,128)S(1)}, f32[8,128]{1,0:T(8,128)S(1)}) custom-call(f32[8,2048]{1,0:T(8,128)S(1)} %get-tuple-element.23.refs_0_, f32[8,256]{1,0:T(8,128)S(1)} %get-tuple-element.24.refs_1_, f32[8,128]{1,0:T(8,128)S(1)} %get-tuple-element.25.refs_2_, ...), custom_call_target="tpu_custom_call" | custom-call | flops 999999995904 | bytes 8595456 | tf_op jit(solution)/shard_map/pallas_call | solution.py:60
  18.0 0.6 collective-permute-start.5
  18.6 0.0 collective-permute-start.4
  18.6 3.9 %collective-permute-start.3 = (bf16[8,2176]{1,0:T(8,128)(2,1)S(1)}, bf16[8,2176]{1,0:T(8,128)(2,1)S(1)}, u32[]{:S(2)}, u32[]{:S(2)}) collective-permute-start(bf16[8,2176]{1,0:T(8,128)(2,1)S(1)} %get-tuple-element.37), channel_id=1, source_target_pairs={{0,4},{4,0},{8,12},{12,8},{1,5},{5,1},{9,13},{13,9},{2,6},{6,2},{1... | collective-permute-start | bytes 104456 | tf_op jit(solution)/shard_map/ppermute | solution.py:33
  22.5 1.3 %collective-permute-done.5.refs_4_ = bf16[8,2176]{1,0:T(8,128)(2,1)S(1)} collective-permute-done((bf16[8,2176]{1,0:T(8,128)(2,1)S(1)}, bf16[8,2176]{1,0:T(8,128)(2,1)S(1)}, u32[]{:S(2)}, u32[]{:S(2)}) %collective-permute-start.5) | collective-permute-done | bytes 34848 | tf_op jit(solution)/shard_map/ppermute | solution.py:33
  23.8 0.6 collective-permute-done.3.refs_2_
  24.4 0.0 copy-start.8
  24.4 0.0 copy-start.11
  24.4 0.0 copy-start.12
  24.4 0.0 copy-start.13
  24.4 0.8 %shard_map.224 = bf16[8,8,1024]{2,1,0:T(8,128)(2,1)S(1)} custom-call(f32[8,2048]{1,0:T(8,128)S(1)} %get-tuple-element.35.refs_0_, f32[8,128]{1,0:T(8,128)S(1)} %get-tuple-element.36.refs_1_, bf16[8,2176]{1,0:T(8,128)(2,1)S(1)} %collective-permute-done.3.refs_2_, bf16[8,2176]{1,0:T(8,128)(2,1)S(1)} %collective-permute-done.4.refs_3_, ...), custom_call_target="tpu_custom_call" | custom-call | flops 999999995904 | bytes 4384768 | tf_op jit(solution)/shard_map/pallas_call | solution.py:60
  25.2 12.0 %all_to_all.15.pieces = bf16[8,8,1024]{2,1,0:T(8,128)(2,1)S(1)} all-to-all(bf16[8,8,1024]{2,1,0:T(8,128)(2,1)S(1)} %shard_map.224), channel_id=1, replica_groups=mesh['rep'=2,'seq'=4,'head'=2,'sub'=2] {'seq','head'}, dimensions={0} | all-to-all | bytes 262144 | tf_op jit(solution)/shard_map/all_to_all | solution.py:38
  37.2 0.0 copy-start.1
  37.3 0.0 copy-start.6
  37.3 0.0 copy-start.7
  37.3 0.0 copy-start.9
  37.3 0.0 copy-start.14
  37.3 0.0 copy-start.15
  37.3 2.5 %shard_map.225 = (f32[8,8,288]{2,1,0:T(8,128)S(1)}, f32[8,1024]{1,0:T(8,128)S(1)}, f32[8,1024]{1,0:T(8,128)S(1)}, f32[8,1024]{1,0:T(8,128)S(1)}) custom-call(bf16[8,8,1024]{2,1,0:T(8,128)(2,1)S(1)} %all_to_all.15.pieces, f32[1,4096]{1,0:T(1,128)S(1)} %bitcast.9, bf16[2,4096,1024]{2,1,0:T(8,128)(2,1)S(1)} %copy-done, f32[4,1024]{1,0:T(4,128)S(1)} %copy-done.12, ...), custom_call_target="tpu_custom_call" | custom-call | flops 999999995904 | bytes 17633280 | tf_op jit(solution)/shard_map/pallas_call | solution.py:60
  39.8 9.7 %all_to_all.16.pieces = f32[8,8,288]{2,1,0:T(8,128)S(1)} all-to-all(f32[8,8,288]{2,1,0:T(8,128)S(1)} %get-tuple-element.39), channel_id=1, replica_groups=mesh['rep'=2,'seq'=4,'head'=2,'sub'=2] {'seq','head'}, dimensions={0} | all-to-all | bytes 147456 | tf_op jit(solution)/shard_map/all_to_all | solution.py:38
  49.5 1.6 %shard_map.226 = (f32[8,16,1024]{2,1,0:T(8,128)}, bf16[8,8,1024]{2,1,0:T(8,128)(2,1)S(1)}) custom-call(f32[8,8,288]{2,1,0:T(8,128)S(1)} %all_to_all.16.pieces, bf16[256,1024]{1,0:T(8,128)(2,1)S(1)} %copy-done.6, f32[1,1024]{1,0:T(1,128)S(1)} %bitcast.11, f32[16,1024]{1,0:T(8,128)S(1)} %copy-done.9, f32[1,1024]{1,0:T(1,128)S(1)} %bitcast.12, ...), custom_call_target="tpu_custom_call" | custom-call | flops 999999995904 | bytes 9650176 | tf_op jit(solution)/shard_map/pallas_call | solution.py:60
  51.1 9.7 %all_to_all.17.pieces = bf16[8,8,1024]{2,1,0:T(8,128)(2,1)S(1)} all-to-all(bf16[8,8,1024]{2,1,0:T(8,128)(2,1)S(1)} %get-tuple-element.42), channel_id=1, replica_groups=mesh['rep'=2,'seq'=4,'head'=2,'sub'=2] {'seq','head'}, dimensions={0} | all-to-all | bytes 262144 | tf_op jit(solution)/shard_map/all_to_all | solution.py:38
  60.9 0.6 %shard_map.227 = bf16[8,1024]{1,0:T(8,128)(2,1)} custom-call(f32[8,1024]{1,0:T(8,128)S(1)} %get-tuple-element.38.mid, bf16[8,8,1024]{2,1,0:T(8,128)(2,1)S(1)} %all_to_all.17.pieces), custom_call_target="tpu_custom_call" | custom-call | flops 999999995904 | bytes 163840 | tf_op jit(solution)/shard_map/pallas_call | solution.py:60
  (22 shorter events, 0.0 us)
Async XLA Ops:
  4.0 11.5 %copy-start.2 = (bf16[8,4,512,128]{3,2,1,0:T(8,128)(2,1)S(1)}, bf16[8,4,512,128]{3,2,1,0:T(8,128)(2,1)}, u32[]{:S(2)}) copy-start(bf16[8,4,512,128]{3,2,1,0:T(8,128)(2,1)} %refs_9_.1) | copy-start | bytes 12582916
  4.0 11.5 %copy-start.3 = (bf16[8,4,512,128]{3,2,1,0:T(8,128)(2,1)S(1)}, bf16[8,4,512,128]{3,2,1,0:T(8,128)(2,1)}, u32[]{:S(2)}) copy-start(bf16[8,4,512,128]{3,2,1,0:T(8,128)(2,1)} %refs_10_.1) | copy-start | bytes 12582916
  4.1 5.7 %collective-permute-start = (bf16[8,2432]{1,0:T(8,128)(2,1)S(1)}, bf16[8,2432]{1,0:T(8,128)(2,1)S(1)}, u32[]{:S(2)}, u32[]{:S(2)}) collective-permute-start(bf16[8,2432]{1,0:T(8,128)(2,1)S(1)} %get-tuple-element.29), channel_id=1, source_target_pairs={{0,4},{4,0},{8,12},{12,8},{1,5},{5,1},{9,13},{13,9},{2,6},{6,2},{1... | collective-permute-start | bytes 116744 | tf_op jit(solution)/shard_map/ppermute | solution.py:33
  7.2 5.6 %collective-permute-start.1 = (bf16[8,2432]{1,0:T(8,128)(2,1)S(1)}, bf16[8,2432]{1,0:T(8,128)(2,1)S(1)}, u32[]{:S(2)}, u32[]{:S(2)}) collective-permute-start(bf16[8,2432]{1,0:T(8,128)(2,1)S(1)} %get-tuple-element.30), channel_id=1, source_target_pairs={{0,8},{4,12},{8,0},{12,4},{1,9},{5,13},{9,1},{13,5},{2,10},{6,14},... | collective-permute-start | bytes 116744 | tf_op jit(solution)/shard_map/ppermute | solution.py:33
  9.8 5.8 %collective-permute-start.2 = (bf16[8,2432]{1,0:T(8,128)(2,1)S(1)}, bf16[8,2432]{1,0:T(8,128)(2,1)S(1)}, u32[]{:S(2)}, u32[]{:S(2)}) collective-permute-start(bf16[8,2432]{1,0:T(8,128)(2,1)S(1)} %get-tuple-element.31), channel_id=1, source_target_pairs={{0,12},{4,8},{8,4},{12,0},{1,13},{5,9},{9,5},{13,1},{2,14},{6,10},... | collective-permute-start | bytes 116744 | tf_op jit(solution)/shard_map/ppermute | solution.py:33
  15.5 8.8 %copy-start.4 = (bf16[2048,1024]{1,0:T(8,128)(2,1)S(1)}, bf16[2048,1024]{1,0:T(8,128)(2,1)}, u32[]{:S(2)}) copy-start(bf16[2048,1024]{1,0:T(8,128)(2,1)} %refs_6_.1) | copy-start | bytes 12582916
  15.5 8.8 %copy-start.10 = (bf16[8,1024]{1,0:T(8,128)(2,1)S(1)}, bf16[8,1024]{1,0:T(8,128)(2,1)}, u32[]{:S(2)}) copy-start(bf16[8,1024]{1,0:T(8,128)(2,1)} %refs_5_.1) | copy-start | bytes 49156
  18.0 5.8 %collective-permute-start.5 = (bf16[8,2176]{1,0:T(8,128)(2,1)S(1)}, bf16[8,2176]{1,0:T(8,128)(2,1)S(1)}, u32[]{:S(2)}, u32[]{:S(2)}) collective-permute-start(bf16[8,2176]{1,0:T(8,128)(2,1)S(1)} %get-tuple-element.37), channel_id=1, source_target_pairs={{0,12},{4,8},{8,4},{12,0},{1,13},{5,9},{9,5},{13,1},{2,14},{6,10},... | collective-permute-start | bytes 104456 | tf_op jit(solution)/shard_map/ppermute | solution.py:33
  18.6 5.2 %collective-permute-start.4 = (bf16[8,2176]{1,0:T(8,128)(2,1)S(1)}, bf16[8,2176]{1,0:T(8,128)(2,1)S(1)}, u32[]{:S(2)}, u32[]{:S(2)}) collective-permute-start(bf16[8,2176]{1,0:T(8,128)(2,1)S(1)} %get-tuple-element.37), channel_id=1, source_target_pairs={{0,8},{4,12},{8,0},{12,4},{1,9},{5,13},{9,1},{13,5},{2,10},{6,14},... | collective-permute-start | bytes 104456 | tf_op jit(solution)/shard_map/ppermute | solution.py:33
  18.6 5.8 %collective-permute-start.3 = (bf16[8,2176]{1,0:T(8,128)(2,1)S(1)}, bf16[8,2176]{1,0:T(8,128)(2,1)S(1)}, u32[]{:S(2)}, u32[]{:S(2)}) collective-permute-start(bf16[8,2176]{1,0:T(8,128)(2,1)S(1)} %get-tuple-element.37), channel_id=1, source_target_pairs={{0,4},{4,0},{8,12},{12,8},{1,5},{5,1},{9,13},{13,9},{2,6},{6,2},{1... | collective-permute-start | bytes 104456 | tf_op jit(solution)/shard_map/ppermute | solution.py:33
  24.4 12.8 %copy-start = (bf16[2,4096,1024]{2,1,0:T(8,128)(2,1)S(1)}, bf16[2,4096,1024]{2,1,0:T(8,128)(2,1)}, u32[]{:S(2)}) copy-start(bf16[2,4096,1024]{2,1,0:T(8,128)(2,1)} %w_in.1) | copy-start | bytes 50331652
  24.4 12.8 %copy-start.5 = (bf16[1024,288]{0,1:T(8,128)(2,1)S(1)}, bf16[1024,288]{0,1:T(8,128)(2,1)}, u32[]{:S(2)}) copy-start(bf16[1024,288]{0,1:T(8,128)(2,1)} %param.37) | copy-start | bytes 1769476
  24.4 12.8 %copy-start.8 = (f32[8,3,1024]{2,0,1:T(8,128)S(1)}, f32[8,3,1024]{2,0,1:T(8,128)}, u32[]{:S(2)}) copy-start(f32[8,3,1024]{2,0,1:T(8,128)} %param.36) | copy-start | bytes 294916
  24.4 12.8 %copy-start.11 = (f32[4096]{0:T(1024)S(1)}, f32[4096]{0:T(1024)}, u32[]{:S(2)}) copy-start(f32[4096]{0:T(1024)} %param.32) | copy-start | bytes 49156
  24.4 12.8 %copy-start.12 = (f32[4,1024]{1,0:T(4,128)S(1)}, f32[4,1024]{1,0:T(4,128)}, u32[]{:S(2)}) copy-start(f32[4,1024]{1,0:T(4,128)} %taps.1) | copy-start | bytes 49156
  24.4 12.8 %copy-start.13 = (f32[1024]{0:T(1024)S(1)}, f32[1024]{0:T(1024)}, u32[]{:S(2)}) copy-start(f32[1024]{0:T(1024)} %param.35) | copy-start | bytes 12292
  37.2 12.3 %copy-start.1 = (bf16[1024,4096]{1,0:T(8,128)(2,1)S(1)}, bf16[1024,4096]{1,0:T(8,128)(2,1)}, u32[]{:S(2)}) copy-start(bf16[1024,4096]{1,0:T(8,128)(2,1)} %w_out.1) | copy-start | bytes 25165828
  37.3 12.2 %copy-start.6 = (bf16[256,1024]{1,0:T(8,128)(2,1)S(1)}, bf16[256,1024]{1,0:T(8,128)(2,1)}, u32[]{:S(2)}) copy-start(bf16[256,1024]{1,0:T(8,128)(2,1)} %w_dt.1) | copy-start | bytes 1572868
  37.3 12.2 %copy-start.7 = (f32[8,16,1024]{2,1,0:T(8,128)S(1)}, f32[8,16,1024]{2,1,0:T(8,128)}, u32[]{:S(2)}) copy-start(f32[8,16,1024]{2,1,0:T(8,128)} %state.1) | copy-start | bytes 1572868
  37.3 12.2 %copy-start.9 = (f32[16,1024]{1,0:T(8,128)S(1)}, f32[16,1024]{1,0:T(8,128)}, u32[]{:S(2)}) copy-start(f32[16,1024]{1,0:T(8,128)} %a_log.1) | copy-start | bytes 196612
  37.3 12.2 %copy-start.14 = (f32[1024]{0:T(1024)S(1)}, f32[1024]{0:T(1024)}, u32[]{:S(2)}) copy-start(f32[1024]{0:T(1024)} %param.39) | copy-start | bytes 12292
  37.3 12.2 %copy-start.15 = (f32[1024]{0:T(1024)S(1)}, f32[1024]{0:T(1024)}, u32[]{:S(2)}) copy-start(f32[1024]{0:T(1024)} %param.41) | copy-start | bytes 12292
